TPU v7x, 32 devices: a whole 2x2x4 slice. The times are simulated.
32 devices in a mesh: grp: 2 (over y), seq: 4 (over z), head: 2 (over x), rep: 2 (over core).
Axes of the slice: x: 2, y: 2, z: 4, core: 2. Of those that a mesh axis runs over, the one named last changes fastest.
Arguments:
- x_proj: bfloat16 [4, 4, 4, 32, 8192], P(('grp', 'rep'), None, 'seq', None, 'head'), parts along dimension 0, may hold values from -6 to 6
- gate_proj: bfloat16 [4, 4, 4, 32, 8192], P(('grp', 'rep'), None, 'seq', None, 'head'), parts along dimension 0, may hold values from -6 to 6
- bc_proj: bfloat16 [4, 4, 4, 32, 256], P(('grp', 'rep'), None, 'seq'), parts along dimension 0, may hold values from -6 to 6
- dt_proj: bfloat16 [4, 4, 4, 32, 128], P(('grp', 'rep'), None, 'seq', None, 'head'), parts along dimension 0, may hold values from -5.5 to 7.5
- a_rate: float32 [128], P('head'), may hold values from 0.0001953125 to 0.05
- dt_bias: float32 [128], P('head'), may hold values from -1 to 1
- d_skip: float32 [128], P('head'), may hold values from 0.5 to 1.5
- conv_x_weight: float32 [4, 8192], P(None, 'head'), may hold values from -3 to 3
- conv_bc_weight: float32 [4, 256], replicated, may hold values from -3 to 3
- norm_gain: float32 [8192], P('head'), may hold values from 0.1 to 1.9
- out_weight: bfloat16 [8192, 2048], P(('seq', 'rep'), 'head'), may hold values from -0.0625 to 0.0625
- request_first_position: int32 [4], P(('grp', 'rep')), parts along dimension 0, may hold values from 0 to 255
- owner: int32 [4, 4], P(('grp', 'rep')), parts along dimension 0, may hold values from 0 to 3, each once within a row
Outputs:
- mixed: bfloat16 [4, 512, 2048], P(('grp', 'rep'), 'seq', 'head'), parts along dimension 0
- ssm_state: float32 [4, 4, 128, 2048], P(('grp', 'rep'), 'seq', 'head'), parts along dimension 0
- conv_x_state: bfloat16 [4, 4, 3, 2048], P(('grp', 'rep'), 'seq', None, 'head'), parts along dimension 0
- conv_bc_state: bfloat16 [4, 4, 3, 64], P(('grp', 'rep'), 'seq'), parts along dimension 0
There are 2 independent parts, one for each index of `grp`. A program takes and returns all parts, laid end to end along the dimension named above; an argument that names none is the same for every part. Nothing has to cross between parts.
Inputs may be any that keep to these rules, and one draw needn't show every extreme that they name: Each row of owner names every index of seq once.
All inputs are finite; a program needn't handle non-finite values.
Results may differ from a plain program's by a relative error of at most 0.007.
Values may be sent and summed in bfloat16 or wider, within the bound.
A program may use at most 128 MiB of HBM per device.

v0:
```python
import jax
import jax.numpy as jnp
from jax import lax
from jax.sharding import PartitionSpec as P

HEAD_DIM = 64
NSTATE = 128
KCONV = 4
SPAN = 128
INNER = 8192
highest = lax.Precision.HIGHEST
stability_constant = 1e-05


def passed_along(value, axis, by):
    devices = lax.axis_size(axis)
    pairs = [(i, i + by) for i in range(devices) if 0 <= i + by < devices]
    return lax.ppermute(value, axis, pairs)


def prefix(value, axis, combine, identity, reverse):
    devices, place = (lax.axis_size(axis), lax.axis_index(axis))
    everything = jax.tree.map(lambda part: lax.all_gather(part, axis), value)
    start = jax.tree.map(
        lambda part, zero: jnp.broadcast_to(jnp.asarray(zero, part.dtype), part.shape),
        value,
        identity,
    )

    def lap(k, before):
        at = devices - 1 - k if reverse else k
        reached = at > place if reverse else at < place
        new = combine(before, jax.tree.map(lambda part: part[at], everything))
        return jax.tree.map(lambda a, b: jnp.where(reached, a, b), new, before)

    return lax.fori_loop(0, devices, lap, start)


def broadcast(block, axis, source):
    block = jnp.where(lax.axis_index(axis) == source, block, jnp.zeros_like(block))
    return lax.psum(block, axis)


def span_terms(x_conv, b_rows, c_rows, step_size, log_decay):
    cum_decay = jnp.cumsum(log_decay, axis=1)
    scores = jnp.einsum("kqn,ktn->kqt", c_rows, b_rows, preferred_element_type=jnp.float32)
    cum_heads = jnp.swapaxes(cum_decay, 1, 2)
    step_heads = jnp.swapaxes(step_size, 1, 2)
    block_len = cum_decay.shape[1]
    causal = jnp.arange(block_len)[:, None] >= jnp.arange(block_len)[None, :]
    decay_gap = cum_heads[:, :, :, None] - cum_heads[:, :, None, :]
    seg_decay = jnp.exp(jnp.where(causal, decay_gap, -jnp.inf))
    weights = (scores[:, None] * seg_decay * step_heads[:, :, None, :]).astype(jnp.bfloat16)
    y_intra = jnp.einsum("khqt,kthp->kqhp", weights, x_conv, preferred_element_type=jnp.float32)
    remaining_length = jnp.exp(cum_decay[:, -1:, :] - cum_decay)
    scaled = ((remaining_length * step_size)[..., None] * x_conv.astype(jnp.float32)).astype(
        jnp.bfloat16
    )
    states = jnp.einsum("kthp,ktn->khpn", scaled, b_rows, preferred_element_type=jnp.float32)
    return (cum_decay, y_intra, states, jnp.exp(cum_decay[:, -1, :]))


def conv_silu(preceding_tokens, current, weight):
    extended = jnp.concatenate([preceding_tokens, current], axis=0)
    length = current.shape[0]
    accum = jnp.zeros(current.shape, jnp.float32)
    for offset in range(weight.shape[0]):
        accum = accum + weight[offset] * extended[offset : offset + length].astype(jnp.float32)
    return jax.nn.silu(accum)


def link(preceding_tokens, later):
    return (
        preceding_tokens[0] * later[0],
        later[0][:, None, None] * preceding_tokens[1] + later[1],
    )


def multiply(preceding_tokens, later):
    return preceding_tokens * later


def add_rows(source, piece):
    return jnp.dot(source, piece, preferred_element_type=jnp.float32)


def take_slab(values, slab_index, seq_count):
    grouped = values.reshape(values.shape[0], seq_count, -1)
    return lax.dynamic_index_in_dim(grouped, slab_index, axis=1, keepdims=False)


def local(
    x_proj,
    gate_proj,
    bc_proj,
    dt_proj,
    a_rate,
    dt_bias,
    d_skip,
    conv_x_weight,
    conv_bc_weight,
    norm_gain,
    out_weight,
    request_first_position,
    owner,
):
    x_all, z_all, bc_all, dt_all = (
        lax.all_to_all(x_proj, "seq", split_axis=1, concat_axis=2, tiled=True),
        lax.all_to_all(gate_proj, "seq", split_axis=1, concat_axis=2, tiled=True),
        lax.all_to_all(bc_proj, "seq", split_axis=1, concat_axis=2, tiled=True),
        lax.all_to_all(dt_proj, "seq", split_axis=1, concat_axis=2, tiled=True),
    )
    tokens_here = x_all.shape[2] * x_all.shape[3]
    x_local = x_all.reshape(tokens_here, x_all.shape[4])
    z_local = z_all.reshape(tokens_here, z_all.shape[4])
    bc_local = bc_all.reshape(tokens_here, bc_all.shape[4])
    dt_local = dt_all.reshape(tokens_here, dt_all.shape[4])
    heads = dt_local.shape[1]
    seq_index = lax.axis_index("seq")
    seq_count = lax.axis_size("seq")
    positions = seq_index * tokens_here + jnp.arange(tokens_here, dtype=jnp.int32)
    is_live = positions >= request_first_position[0]
    x_live = jnp.where(is_live[:, None], x_local, jnp.zeros_like(x_local))
    bc_live = jnp.where(is_live[:, None], bc_local, jnp.zeros_like(bc_local))
    rim_rows = KCONV - 1
    tail_x = x_live[tokens_here - rim_rows :]
    tail_bc = bc_live[tokens_here - rim_rows :]
    before_x, before_bc = passed_along((tail_x, tail_bc), "seq", 1)
    x_conv = conv_silu(before_x, x_live, conv_x_weight).astype(jnp.bfloat16)
    bc_conv = conv_silu(before_bc, bc_live, conv_bc_weight).astype(jnp.bfloat16)
    step_size = (
        jax.nn.softplus(dt_local.astype(jnp.float32) + dt_bias)
        * is_live.astype(jnp.float32)[:, None]
    )
    log_decay = -a_rate * step_size
    blocks = tokens_here // SPAN
    x_blocks = x_conv.reshape(blocks, SPAN, heads, HEAD_DIM)
    b_blocks = bc_conv[:, :NSTATE].reshape(blocks, SPAN, NSTATE)
    c_blocks = bc_conv[:, NSTATE:].reshape(blocks, SPAN, NSTATE)
    cum_decay, y_intra, states, decays = span_terms(
        x_blocks,
        b_blocks,
        c_blocks,
        step_size.reshape(blocks, SPAN, heads),
        log_decay.reshape(blocks, SPAN, heads),
    )

    def advance(carry, inputs):
        factor, contrib = inputs
        return (factor[:, None, None] * carry + contrib, carry)

    zero_state = jnp.zeros((heads, HEAD_DIM, NSTATE), jnp.float32)
    local_final, local_enter = lax.scan(advance, zero_state, (decays, states))
    dev_decay = jnp.prod(decays, axis=0)
    ones_heads = jnp.ones((heads,), jnp.float32)
    enter_decay, enter_state = prefix(
        (dev_decay, local_final), "seq", link, (ones_heads, zero_state), False
    )
    c_wide = c_blocks.astype(jnp.float32)
    before_block = jnp.concatenate([ones_heads[None], jnp.cumprod(decays, axis=0)[:-1]], axis=0)
    entering = local_enter + before_block[:, :, None, None] * enter_state[None]
    y_state = jnp.exp(cum_decay)[..., None] * jnp.einsum(
        "kqn,khpn->kqhp", c_wide, entering, precision=highest
    )
    y_total = y_intra + y_state + d_skip[:, None] * x_blocks.astype(jnp.float32)
    y_flat = y_total.reshape(tokens_here, heads * HEAD_DIM)
    gated = y_flat * jax.nn.silu(z_local.astype(jnp.float32))
    square_sums = lax.psum(jnp.sum(gated * gated, axis=1), "head")
    normed = (
        gated * lax.rsqrt(square_sums[:, None] / INNER + stability_constant) * norm_gain
    ).astype(jnp.bfloat16)
    last_index = seq_count - 1
    after_decay = prefix(dev_decay, "seq", multiply, ones_heads, True)
    final_state = lax.psum(after_decay[:, None, None] * local_final, "seq")
    keep_x, keep_bc = (broadcast(tail_x, "seq", last_index), broadcast(tail_bc, "seq", last_index))
    slab_index = jnp.sum(
        jnp.where(owner[0] == seq_index, jnp.arange(seq_count, dtype=jnp.int32), 0)
    )
    ssm_state = take_slab(final_state.reshape(heads, -1), slab_index, seq_count)[None, None]
    conv_x_state = take_slab(keep_x, slab_index, seq_count)[None, None]
    conv_bc_state = take_slab(keep_bc, slab_index, seq_count)[None, None]
    features = lax.all_gather(normed, "head", axis=1, tiled=True)
    out_cols = out_weight.shape[1]
    mixed_sum = add_rows(features, lax.all_gather(out_weight, ("seq", "rep"), axis=0, tiled=True))
    mixed = mixed_sum.astype(jnp.bfloat16).reshape(1, tokens_here, out_cols)
    return (mixed, ssm_state, conv_x_state, conv_bc_state)


def solution(mesh):
    return jax.shard_map(
        local,
        mesh=mesh,
        in_specs=(
            P(("grp", "rep"), None, "seq", None, "head"),
            P(("grp", "rep"), None, "seq", None, "head"),
            P(("grp", "rep"), None, "seq", None, None),
            P(("grp", "rep"), None, "seq", None, "head"),
            P("head"),
            P("head"),
            P("head"),
            P(None, "head"),
            P(),
            P("head"),
            P(("seq", "rep"), "head"),
            P(("grp", "rep")),
            P(("grp", "rep"), None),
        ),
        out_specs=(
            P(("grp", "rep"), "seq", "head"),
            P(("grp", "rep"), "seq", "head", None),
            P(("grp", "rep"), "seq", None, "head"),
            P(("grp", "rep"), "seq", None, None),
        ),
        check_vma=False,
    )
```

profile of v0, /device:TPU:0, one launch (start us, length us, event | category | flops | bytes accessed | tf_op | source)
XLA Modules:
  0.0 532.8 jit_solution(8478039113186121479)
XLA Ops:
  7.2 0.7 copy-done
  7.9 0.7 reshape.454
  8.6 6.3 %all-to-all-start.2 = ((bf16[4,2,1024]{2,1,0:T(2,128)(2,1)}), bf16[4,2,1024]{2,1,0:T(2,128)(2,1)S(1)}, u32[]{:S(2)}, u32[]{:S(2)}) async-start(bf16[4,2,1024]{2,1,0:T(2,128)(2,1)} %reshape.454), calls=%async_computation.2 | async-start | bytes 32768 | tf_op jit(solution)/shard_map/all_to_all | solution.py:111
  15.6 1.7 fusion.36
  17.3 1.4 fusion.37
  18.7 0.6 fusion.35
  19.3 0.7 neg.47
  20.0 0.6 all-to-all-done.2
  20.6 4.5 all-to-all-start.1
  25.2 0.7 broadcast_multiply_fusion.1
  25.9 0.2 reduce_window_sum.13
  26.1 0.7 bitcast_exponential_fusion
  26.9 0.2 mul.344
  27.1 1.9 copy.80
  29.0 11.5 %all-gather = f32[4,1,64]{2,1,0:T(1,128)S(1)} all-gather(f32[1,1,64]{2,1,0:T(1,128)S(1)} %get-tuple-element.290), channel_id=2, replica_groups=mesh['grp'=2,'seq'=4,'head'=2,'rep'=2] {'seq'}, dimensions={0}, use_global_device_ids=true | all-gather | bytes 1280 | tf_op jit(solution)/shard_map/all_gather | solution.py:23
  40.5 3.7 all-to-all-start
  44.2 0.6 exponential_multiply_fusion
  44.8 0.1 while.36
  45.0 0.9 bitcast_select_fusion.1
  46.0 0.6 broadcast_select_fusion.3
  46.6 3.8 collective-permute-start.1
  50.4 16.6 %all-to-all-done = bf16[1,4,1,32,4096]{4,3,2,0,1:T(8,128)(2,1)S(1)} async-done(((bf16[1,4,1,32,4096]{4,3,2,0,1:T(8,128)(2,1)}), bf16[1,4,1,32,4096]{4,3,2,0,1:T(8,128)(2,1)S(1)}, u32[]{:S(2)}, u32[]{:S(2)}) %all-to-all-start) | async-done | bytes 1048608 | tf_op jit(solution)/shard_map/all_to_all | solution.py:108
  67.0 0.2 bitcast_select_fusion
  67.3 1.3 collective-permute-start
  68.6 0.6 copy-done.16
  69.2 0.9 multiply_convert_fusion.4
  70.2 3.1 multiply_convert_fusion.2
  73.3 1.6 copy.81
  74.9 2.4 broadcast_multiply_fusion
  77.3 5.7 %all-to-all-start.3 = ((bf16[1,4,1,32,4096]{4,3,2,0,1:T(8,128)(2,1)}), bf16[1,4,1,32,4096]{4,3,2,0,1:T(8,128)(2,1)}, u32[]{:S(2)}, u32[]{:S(2)}) async-start(bf16[1,4,1,32,4096]{4,3,2,0,1:T(8,128)(2,1)} %bitcast.35), calls=%async_computation.3 | async-start | bytes 2097152 | tf_op jit(solution)/shard_map/all_to_all | solution.py:109
  83.5 48.3 %all-to-all-done.3 = bf16[1,4,1,32,4096]{4,3,2,0,1:T(8,128)(2,1)} async-done(((bf16[1,4,1,32,4096]{4,3,2,0,1:T(8,128)(2,1)}), bf16[1,4,1,32,4096]{4,3,2,0,1:T(8,128)(2,1)}, u32[]{:S(2)}, u32[]{:S(2)}) %all-to-all-start.3) | async-done | bytes 1048608 | tf_op jit(solution)/shard_map/all_to_all | solution.py:109
  131.8 2.7 bitcast_convert_fusion
  134.6 4.6 reshape.449
  139.2 4.8 copy.87
  144.0 1.3 copy.72
  145.3 1.7 copy.82
  147.0 3.0 reshape_reshape.3
  150.0 1.1 copy-done.4
  151.2 3.3 fusion.1
  154.4 87.4 %all-gather.10.cloned.1.call-done = f32[256,64,128]{2,1,0:T(8,128)} async-done(((f32[64,64,128]{2,1,0:T(8,128)}), f32[256,64,128]{2,1,0:T(8,128)}) %all-gather.10.cloned.1.call-update) | async-done | bytes 8388624 | tf_op jit(solution)/shard_map/all_gather | solution.py:23
  241.9 11.4 %while.35 = (s32[]{:T(128)}, f32[64,64,128]{2,1,0:T(8,128)S(1)}, s32[]{:T(128)}, f32[4,64]{1,0:T(4,128)}, f32[4,64,64,128]{3,2,1,0:T(8,128)}, /*index=5*/s32[]{:T(128)}, s32[]{:T(128)}) while((s32[]{:T(128)}, f32[64,64,128]{2,1,0:T(8,128)S(1)}, s32[]{:T(128)}, f32[4,64]{1,0:T(4,128)}, f32[4,64,64,128]{3,2,1,0:T(8,128)}, ...), condition=%wide.region_2.3_spmd.clone, body=%wide.region_1.2_spmd.clone.sunk | while | flops 2097156 | bytes 6292329 | solution.py:36
  241.9 0.7 dynamic-slice_bitcast_fusion.4
  242.6 2.1 fusion.44
  244.7 0.7 dynamic-slice_bitcast_fusion.4
  245.3 2.1 fusion.44
  247.4 0.7 dynamic-slice_bitcast_fusion.4
  248.1 2.3 fusion.44
  250.4 0.7 dynamic-slice_bitcast_fusion.4
  251.1 2.1 fusion.44
  253.2 5.9 %multiply_reduce_fusion = (f32[128]{0:T(128)S(1)}, f32[1,128,64,64]{1,3,2,0:T(8,128)}) fusion(f32[1,128,64,64]{1,3,2,0:T(8,128)} %copy.87, f32[1,128,64,64]{1,3,2,0:T(8,128)} %bitcast.133, f32[64]{0:T(128)S(1)} %copy-done.18, f32[64,64,128]{2,1,0:T(8,128)S(1)} %get-tuple-element.223, bf16[128,256]{1,0:T(8,128)(2,1)S(1)} %multiply_convert_fusion.4, ...), kind=kOutput, calls=%fused_computation.17 | convolution fusion | flops 811073408 | bytes 10552320 | tf_op jit(solution)/shard_map/kqn,khpn->kqhp/dot_general | solution.py:162
  259.1 3.1 copy.85
  262.2 4.9 psum.28
  267.1 3.3 fusion.14
  270.5 0.5 all-gather.8.cloned.1.call-update
  271.1 0.6 fusion.33
  273.7 18.3 %all-reduce = (bf16[3,4,1024]{2,0,1:T(4,128)(2,1)S(1)}, bf16[3,4,64]{2,0,1:T(4,128)(2,1)S(1)}) all-reduce(bf16[3,4,1024]{2,0,1:T(4,128)(2,1)S(1)} %bitcast.140, bf16[3,4,64]{2,0,1:T(4,128)(2,1)S(1)} %copy.89), channel_id=1, replica_groups=mesh['grp'=2,'seq'=4,'head'=2,'rep'=2] {'seq'}, use_global_device_ids=true, to_apply=%region_9.10 | all-reduce | flops 13056 | bytes 52224 | tf_op jit(solution)/shard_map/psum | solution.py:41
  292.1 0.6 dynamic-slice_bitcast_fusion.2
  292.6 0.6 dynamic-slice_bitcast_fusion.1
  293.2 37.3 %all-reduce.3.cloned.1.call-done = f32[64,4,2048]{2,1,0:T(4,128)} async-done(((f32[64,4,2048]{2,1,0:T(4,128)}), f32[64,4,2048]{2,1,0:T(4,128)}) %all-reduce.3.cloned.1.call-update) | async-done | bytes 2097168 | tf_op jit(solution)/shard_map/psum | solution.py:174
  330.5 2.1 constant_dynamic-slice_fusion
  332.7 1.0 copy.92
  333.6 30.6 %all-gather.6.cloned.1.call-done = bf16[128,8192]{1,0:T(8,128)(2,1)} async-done(((bf16[128,4096]{1,0:T(8,128)(2,1)}), bf16[128,8192]{1,0:T(8,128)(2,1)}) %all-gather.6.cloned.1.call-update) | async-done | bytes 2097168 | tf_op jit(solution)/shard_map/all_gather | solution.py:182
  364.2 152.6 %all-gather.8.cloned.1.call-done = bf16[8192,1024]{1,0:T(8,128)(2,1)} async-done(((bf16[1024,1024]{1,0:T(8,128)(2,1)}), bf16[8192,1024]{1,0:T(8,128)(2,1)}) %all-gather.8.cloned.1.call-update) | async-done | bytes 16777232 | tf_op jit(solution)/shard_map/all_gather | solution.py:184
  516.8 9.5 %fusion.16 = bf16[1,128,1024]{2,1,0:T(8,128)(2,1)} fusion(bf16[128,8192]{1,0:T(8,128)(2,1)} %all-gather.6.cloned.1.call-done, bf16[8192,1024]{1,0:T(8,128)(2,1)} %all-gather.8.cloned.1.call-done), kind=kOutput, calls=%fused_computation.31 | convolution fusion | flops 2147614720 | bytes 19136512 | tf_op jit(solution)/shard_map/dot_general | solution.py:84
  (67 shorter events, 1.2 us)
Async XLA Ops:
  7.2 0.8 copy-start
  8.6 12.0 %all-to-all-start.2 = ((bf16[4,2,1024]{2,1,0:T(2,128)(2,1)}), bf16[4,2,1024]{2,1,0:T(2,128)(2,1)S(1)}, u32[]{:S(2)}, u32[]{:S(2)}) async-start(bf16[4,2,1024]{2,1,0:T(2,128)(2,1)} %reshape.454), calls=%async_computation.2 | async-start | bytes 32768 | tf_op jit(solution)/shard_map/all_to_all | solution.py:111
  19.3 7.5 %copy-start.11 = (f32[128]{0:T(128)}, f32[128]{0:T(128)S(1)}, u32[]{:S(2)}) copy-start(f32[128]{0:T(128)S(1)} %get-tuple-element.282) | copy-start | bytes 1540
  20.6 19.9 %all-to-all-start.1 = ((bf16[1,4,1,32,256]{4,3,2,0,1:T(8,128)(2,1)}), bf16[1,4,1,32,256]{4,3,2,0,1:T(8,128)(2,1)S(1)}, u32[]{:S(2)}, u32[]{:S(2)}) async-start(bf16[1,4,1,32,256]{4,3,2,0,1:T(8,128)(2,1)} %bitcast.145), calls=%async_computation.1 | async-start | bytes 131072 | tf_op jit(solution)/shard_map/all_to_all | solution.py:110
  29.0 15.8 %copy-start.6 = (f32[64]{0:T(128)S(1)}, f32[64]{0:T(128)}, u32[]{:S(2)}) copy-start(f32[64]{0:T(128)} %custom-call.1) | copy-start | bytes 772
  29.0 16.0 %copy-start.15 = (pred[128]{0:T(512)(128)(4,1)S(1)}, pred[128]{0:T(512)(128)(4,1)}, u32[]{:S(2)}) copy-start(pred[128]{0:T(512)(128)(4,1)} %get-tuple-element.283) | copy-start | bytes 388
  40.5 4.5 copy-start.5
  40.5 29.6 %copy-start.3 = (f32[128,4096]{1,0:T(8,128)S(1)}, f32[128,4096]{1,0:T(8,128)}, u32[]{:S(2)}) copy-start(f32[128,4096]{1,0:T(8,128)} %copy.80) | copy-start | bytes 6291460
  40.5 26.5 %all-to-all-start = ((bf16[1,4,1,32,4096]{4,3,2,0,1:T(8,128)(2,1)}), bf16[1,4,1,32,4096]{4,3,2,0,1:T(8,128)(2,1)S(1)}, u32[]{:S(2)}, u32[]{:S(2)}) async-start(bf16[1,4,1,32,4096]{4,3,2,0,1:T(8,128)(2,1)} %bitcast.135), calls=%async_computation | async-start | bytes 2097152 | tf_op jit(solution)/shard_map/all_to_all | solution.py:108
  44.2 197.7 %all-gather.10.cloned.1.call-start = ((), (), s32[]{:S(2)}) async-start(), calls=%async_computation.7 | async-start | bytes 10485760 | tf_op jit(solution)/shard_map/all_gather | solution.py:23
  45.0 22.0 %copy-start.7 = (f32[64]{0:T(128)}, f32[64]{0:T(128)S(1)}, u32[]{:S(2)}) copy-start(f32[64]{0:T(128)S(1)} %get-tuple-element.224) | copy-start | bytes 772
  45.0 22.0 %copy-start.10 = (f32[4,64]{1,0:T(4,128)}, f32[4,64]{1,0:T(4,128)S(1)}, u32[]{:S(2)}) copy-start(f32[4,64]{1,0:T(4,128)S(1)} %get-tuple-element.430) | copy-start | bytes 3076
  46.6 22.0 %collective-permute-start.1 = (bf16[3,256]{1,0:T(4,128)(2,1)S(1)}, bf16[3,256]{1,0:T(4,128)(2,1)S(1)}, u32[]{:S(2)}, u32[]{:S(2)}) collective-permute-start(bf16[3,256]{1,0:T(4,128)(2,1)S(1)} %get-tuple-element.287), channel_id=1, source_target_pairs={{0,4},{4,8},{8,12},{1,5},{5,9},{9,13},{2,6},{6,10},{10,14},{3,7},{... | collective-permute-start | bytes 4616 | tf_op jit(solution)/shard_map/ppermute | solution.py:18
  67.3 2.9 collective-permute-start
  68.6 0.6 copy-start.16
  73.3 1.6 copy-start.8
  73.3 1.6 copy-start.17
  77.3 5.7 %copy-start.12 = (f32[128]{0:T(128)S(1)}, f32[128]{0:T(128)}, u32[]{:S(2)}) copy-start(f32[128]{0:T(128)} %copy-done.11) | copy-start | bytes 1540
  77.3 5.8 %copy-start.14 = (f32[64]{0:T(128)S(1)}, f32[64]{0:T(128)}, u32[]{:S(2)}) copy-start(f32[64]{0:T(128)} %param.22) | copy-start | bytes 772
  77.3 54.5 %all-to-all-start.3 = ((bf16[1,4,1,32,4096]{4,3,2,0,1:T(8,128)(2,1)}), bf16[1,4,1,32,4096]{4,3,2,0,1:T(8,128)(2,1)}, u32[]{:S(2)}, u32[]{:S(2)}) async-start(bf16[1,4,1,32,4096]{4,3,2,0,1:T(8,128)(2,1)} %bitcast.35), calls=%async_computation.3 | async-start | bytes 2097152 | tf_op jit(solution)/shard_map/all_to_all | solution.py:109
  83.0 247.5 %all-reduce.3.cloned.1.call-start = ((), (), s32[]{:S(2)}) async-start(), calls=%async_computation.6 | async-start | bytes 4194304 | tf_op jit(solution)/shard_map/psum | solution.py:174
  149.9 1.2 copy-start.4
  150.0 214.3 %all-gather.6.cloned.1.call-start = ((), (), s32[]{:S(2)}) async-start(), calls=%async_computation.4 | async-start | bytes 3145728 | tf_op jit(solution)/shard_map/all_gather | solution.py:182
  241.9 11.4 %copy-start.18 = (f32[64]{0:T(128)S(1)}, f32[64]{0:T(128)}, u32[]{:S(2)}) copy-start(f32[64]{0:T(128)} %param.23) | copy-start | bytes 772
  259.1 8.0 %copy-start.2 = (f32[1,4,1,32,4096]{4,3,1,2,0:T(8,128)S(1)}, f32[1,4,1,32,4096]{4,3,1,2,0:T(8,128)}, u32[]{:S(2)}) copy-start(f32[1,4,1,32,4096]{4,3,1,2,0:T(8,128)} %bitcast_convert_fusion) | copy-start | bytes 6291460
  259.1 8.0 %copy-start.9 = (f32[4096]{0:T(1024)S(1)}, f32[4096]{0:T(1024)}, u32[]{:S(2)}) copy-start(f32[4096]{0:T(1024)} %param.26) | copy-start | bytes 49156
  270.4 0.7 copy-start.19
  270.4 3.2 copy-start.13
  270.4 246.4 %all-gather.8.cloned.1.call-start = ((), (), s32[]{:S(2)}) async-start(), calls=%async_computation.5 | async-start | bytes 18874368 | tf_op jit(solution)/shard_map/all_gather | solution.py:184
  516.8 9.5 %copy-start.1 = (bf16[1,4,1,32,64]{4,3,2,1,0:T(8,128)(2,1)S(1)}, bf16[1,4,1,32,64]{4,3,2,1,0:T(8,128)(2,1)}, u32[]{:S(2)}) copy-start(bf16[1,4,1,32,64]{4,3,2,1,0:T(8,128)(2,1)} %param.20) | copy-start | bytes 49156
Sparse Core Ops, SparseCore 0:
  77.4 164.3 all-gather.9
  244.2 86.2 all-reduce.2
  332.1 32.1 all-gather.5
  365.7 151.0 all-gather.7
where the time goes:
time: 534 us; the launch traced here: 533 us
  waiting for transfers between devices  374 us (70%)
  local copies, waits for them, and re-layouts  36.1 us (7%)
  blocking collectives  34.7 us (6%)
  starting transfers between devices  25.4 us (5%)
  other arithmetic  24.6 us (5%)
  matrix products  21.1 us (4%)
  between operations  16.6 us (3%)
    all_gather x1, waiting for transfers between devices, local(): lax.all_gather(out_weight, ('seq', 'rep'), axis=0, tiled=True)  153 us
    all_gather x1, waiting for transfers between devices, prefix(): everything = jax.tree.map(lambda part: lax.all_gather(part, axis), value)  87.4 us
    all_to_all x1, waiting for transfers between devices, local(): lax.all_to_all(gate_proj, 'seq', split_axis=1, concat_axis=2, tiled=True)  48.3 us
    psum x1, waiting for transfers between devices, local(): final_state = lax.psum(after_decay[:, None, None] * local_final, 'seq')  37.3 us
    all_gather x1, waiting for transfers between devices, local(): features = lax.all_gather(normed, 'head', axis=1, tiled=True)  30.6 us
    psum x1, blocking collectives, broadcast(): return lax.psum(block, axis)  18.3 us
    all_to_all x1, waiting for transfers between devices, local(): lax.all_to_all(x_proj, 'seq', split_axis=1, concat_axis=2, tiled=True)  16.6 us
    all_gather x1, blocking collectives, prefix(): everything = jax.tree.map(lambda part: lax.all_gather(part, axis), value)  11.5 us
  transfers between devices with their start and end apart: 10, of which 8 were waited for; matrix products, arithmetic and copies ran while one was open for 12% of the time, Pallas kernels for 0%

commit v1 on v0

--- a/solution.py
+++ b/solution.py
@@ -171,7 +171,7 @@
     ).astype(jnp.bfloat16)
     last_index = seq_count - 1
     after_decay = prefix(dev_decay, "seq", multiply, ones_heads, True)
-    final_state = lax.psum(after_decay[:, None, None] * local_final, "seq")
+    final_state = jnp.sum(lax.all_gather(after_decay[:, None, None] * local_final, "seq"), axis=0)
     keep_x, keep_bc = (broadcast(tail_x, "seq", last_index), broadcast(tail_bc, "seq", last_index))
     slab_index = jnp.sum(
         jnp.where(owner[0] == seq_index, jnp.arange(seq_count, dtype=jnp.int32), 0)

time: 534 us -> 597 us (1.12)
  waiting for transfers between devices: 374 us -> 423 us
  blocking collectives: 34.7 us -> 45.5 us
    all_gather x0 -> x1, waiting for transfers between devices: none -> 88.9 us  [local(): lax.all_gather(after_decay[:, None, None] * local_final, 'seq')]
    psum x1 -> x0, waiting for transfers between devices: 37.3 us -> none  [local(): final_state = lax.psum(after_decay[:, None, None] * local_final, 'seq')]
    psum x1, blocking collectives: 18.3 us -> 29.1 us  [broadcast(): return lax.psum(block, axis)]
    all_gather x1, waiting for transfers between devices: 30.6 us -> 23.3 us  [local(): features = lax.all_gather(normed, 'head', axis=1, tiled=True)]
  transfers between devices with their start and end apart: 10 -> 10, of which waited for: 8 -> 8; matrix products, arithmetic and copies ran while one was open for 12% -> 11% of each run, Pallas kernels for 0% -> 0%
where the time goes in v1:
time: 597 us; the launch traced here: 596 us
  waiting for transfers between devices  423 us (71%)
  blocking collectives  45.5 us (8%)
  local copies, waits for them, and re-layouts  33.9 us (6%)
  other arithmetic  29.4 us (5%)
  starting transfers between devices  25.4 us (4%)
  matrix products  22.3 us (4%)
  between operations  16.6 us (3%)
    all_gather x1, waiting for transfers between devices, local(): lax.all_gather(out_weight, ('seq', 'rep'), axis=0, tiled=True)  153 us
    all_gather x1, waiting for transfers between devices, prefix(): everything = jax.tree.map(lambda part: lax.all_gather(part, axis), value)  91 us
    all_gather x1, waiting for transfers between devices, local(): lax.all_gather(after_decay[:, None, None] * local_final, 'seq')  88.9 us
    all_to_all x1, waiting for transfers between devices, local(): lax.all_to_all(gate_proj, 'seq', split_axis=1, concat_axis=2, tiled=True)  48.3 us
    psum x1, blocking collectives, broadcast(): return lax.psum(block, axis)  29.1 us
    all_gather x1, waiting for transfers between devices, local(): features = lax.all_gather(normed, 'head', axis=1, tiled=True)  23.3 us
    all_to_all x1, waiting for transfers between devices, local(): lax.all_to_all(x_proj, 'seq', split_axis=1, concat_axis=2, tiled=True)  16.7 us
  transfers between devices with their start and end apart: 10, of which 8 were waited for; matrix products, arithmetic and copies ran while one was open for 11% of the time, Pallas kernels for 0%

profile of v1, /device:TPU:0, one launch (start us, length us, event | category | flops | bytes accessed | tf_op | source)
XLA Modules:
  0.0 595.8 jit_solution(2211833884249454582)
XLA Ops:
  7.2 0.7 copy-done
  7.9 0.7 reshape.457
  8.6 6.3 %all-to-all-start.2 = ((bf16[4,2,1024]{2,1,0:T(2,128)(2,1)}), bf16[4,2,1024]{2,1,0:T(2,128)(2,1)S(1)}, u32[]{:S(2)}, u32[]{:S(2)}) async-start(bf16[4,2,1024]{2,1,0:T(2,128)(2,1)} %reshape.457), calls=%async_computation.2 | async-start | bytes 32768 | tf_op jit(solution)/shard_map/all_to_all | solution.py:111
  15.6 1.7 fusion.36
  17.3 1.4 fusion.37
  18.7 0.6 fusion.35
  19.3 0.7 neg.47
  20.0 0.6 all-to-all-done.2
  20.6 4.5 all-to-all-start.1
  25.2 0.7 broadcast_multiply_fusion.1
  25.9 0.2 reduce_window_sum.13
  26.1 0.7 bitcast_exponential_fusion
  26.9 0.2 mul.348
  27.1 1.8 copy.80
  28.9 11.5 %all-gather = f32[4,1,64]{2,1,0:T(1,128)S(1)} all-gather(f32[1,1,64]{2,1,0:T(1,128)S(1)} %get-tuple-element.290), channel_id=2, replica_groups=mesh['grp'=2,'seq'=4,'head'=2,'rep'=2] {'seq'}, dimensions={0}, use_global_device_ids=true | all-gather | bytes 1280 | tf_op jit(solution)/shard_map/all_gather | solution.py:23
  40.4 3.7 all-to-all-start
  44.1 0.5 exponential_multiply_fusion
  44.9 0.9 bitcast_select_fusion.1
  45.8 0.6 broadcast_select_fusion.3
  46.4 3.8 collective-permute-start.1
  50.2 16.7 %all-to-all-done = bf16[1,4,1,32,4096]{4,3,2,0,1:T(8,128)(2,1)S(1)} async-done(((bf16[1,4,1,32,4096]{4,3,2,0,1:T(8,128)(2,1)}), bf16[1,4,1,32,4096]{4,3,2,0,1:T(8,128)(2,1)S(1)}, u32[]{:S(2)}, u32[]{:S(2)}) %all-to-all-start) | async-done | bytes 1048608 | tf_op jit(solution)/shard_map/all_to_all | solution.py:108
  66.9 0.2 bitcast_select_fusion
  67.2 1.3 collective-permute-start
  68.5 0.6 copy-done.15
  69.1 0.9 multiply_convert_fusion.4
  70.1 3.1 multiply_convert_fusion.2
  73.1 1.6 copy.81
  74.8 2.4 broadcast_multiply_fusion
  77.3 0.7 all-gather.14.cloned.1.call-update
  78.0 5.7 all-to-all-start.3
  84.2 48.3 %all-to-all-done.3 = bf16[1,4,1,32,4096]{4,3,2,0,1:T(8,128)(2,1)} async-done(((bf16[1,4,1,32,4096]{4,3,2,0,1:T(8,128)(2,1)}), bf16[1,4,1,32,4096]{4,3,2,0,1:T(8,128)(2,1)}, u32[]{:S(2)}, u32[]{:S(2)}) %all-to-all-start.3) | async-done | bytes 1048608 | tf_op jit(solution)/shard_map/all_to_all | solution.py:109
  132.5 2.7 bitcast_convert_fusion
  135.2 4.7 reshape.451
  139.9 4.8 copy.87
  144.7 1.3 copy.72
  146.0 1.7 copy.82
  147.7 3.9 fusion.1
  151.6 91.0 %all-gather.12.cloned.1.call-done = f32[256,64,128]{2,1,0:T(8,128)} async-done(((f32[64,64,128]{2,1,0:T(8,128)}), f32[256,64,128]{2,1,0:T(8,128)}) %all-gather.12.cloned.1.call-update) | async-done | bytes 8388624 | tf_op jit(solution)/shard_map/all_gather | solution.py:23
  242.6 11.7 %while.35 = (s32[]{:T(128)}, f32[64,64,128]{2,1,0:T(8,128)S(1)}, s32[]{:T(128)}, f32[4,64]{1,0:T(4,128)}, f32[4,64,64,128]{3,2,1,0:T(8,128)}, /*index=5*/s32[]{:T(128)}, s32[]{:T(128)}) while((s32[]{:T(128)}, f32[64,64,128]{2,1,0:T(8,128)S(1)}, s32[]{:T(128)}, f32[4,64]{1,0:T(4,128)}, f32[4,64,64,128]{3,2,1,0:T(8,128)}, ...), condition=%wide.region_2.3_spmd.clone, body=%wide.region_1.2_spmd.clone.sunk | while | flops 2097156 | bytes 6292329 | solution.py:36
  242.6 0.7 dynamic-slice_bitcast_fusion.4
  243.3 2.1 fusion.44
  245.4 0.7 dynamic-slice_bitcast_fusion.4
  246.0 2.1 fusion.44
  248.1 0.7 dynamic-slice_bitcast_fusion.4
  248.8 2.3 fusion.44
  251.2 0.7 dynamic-slice_bitcast_fusion.4
  251.9 2.3 fusion.44
  254.3 6.4 %multiply_reduce_fusion = (f32[128]{0:T(128)S(1)}, f32[1,128,64,64]{1,3,2,0:T(8,128)}) fusion(f32[1,128,64,64]{1,3,2,0:T(8,128)} %copy.87, f32[1,128,64,64]{1,3,2,0:T(8,128)} %bitcast.135, f32[64]{0:T(128)S(1)} %copy-done.17, f32[64,64,128]{2,1,0:T(8,128)S(1)} %get-tuple-element.223, bf16[128,256]{1,0:T(8,128)(2,1)S(1)} %multiply_convert_fusion.4, ...), kind=kOutput, calls=%fused_computation.17 | convolution fusion | flops 811073408 | bytes 10552320 | tf_op jit(solution)/shard_map/kqn,khpn->kqhp/dot_general | solution.py:162
  260.7 3.1 copy.85
  263.7 4.9 psum.21
  268.6 3.3 fusion.14
  272.0 0.5 all-gather.10.cloned.1.call-update
  272.6 0.6 fusion.33
  275.2 29.1 %all-reduce = (bf16[3,4,1024]{2,0,1:T(4,128)(2,1)S(1)}, bf16[3,4,64]{2,0,1:T(4,128)(2,1)S(1)}) all-reduce(bf16[3,4,1024]{2,0,1:T(4,128)(2,1)S(1)} %bitcast.142, bf16[3,4,64]{2,0,1:T(4,128)(2,1)S(1)} %copy.89), channel_id=1, replica_groups=mesh['grp'=2,'seq'=4,'head'=2,'rep'=2] {'seq'}, use_global_device_ids=true, to_apply=%region_9.10 | all-reduce | flops 13056 | bytes 52224 | tf_op jit(solution)/shard_map/psum | solution.py:41
  304.3 0.6 dynamic-slice_bitcast_fusion.2
  304.9 0.6 dynamic-slice_bitcast_fusion.1
  305.5 88.9 %all-gather.14.cloned.1.call-done = f32[256,64,128]{2,1,0:T(8,128)} async-done(((f32[64,64,128]{2,1,0:T(8,128)}), f32[256,64,128]{2,1,0:T(8,128)}) %all-gather.14.cloned.1.call-update) | async-done | bytes 8388624 | tf_op jit(solution)/shard_map/all_gather | solution.py:174
  394.3 4.6 reduce_sum.28
  398.9 1.7 reshape_reshape.3
  400.6 2.4 constant_dynamic-slice_fusion
  403.0 1.0 copy.92
  404.0 23.3 %all-gather.8.cloned.1.call-done = bf16[128,8192]{1,0:T(8,128)(2,1)} async-done(((bf16[128,4096]{1,0:T(8,128)(2,1)}), bf16[128,8192]{1,0:T(8,128)(2,1)}) %all-gather.8.cloned.1.call-update) | async-done | bytes 2097168 | tf_op jit(solution)/shard_map/all_gather | solution.py:182
  427.2 152.6 %all-gather.10.cloned.1.call-done = bf16[8192,1024]{1,0:T(8,128)(2,1)} async-done(((bf16[1024,1024]{1,0:T(8,128)(2,1)}), bf16[8192,1024]{1,0:T(8,128)(2,1)}) %all-gather.10.cloned.1.call-update) | async-done | bytes 16777232 | tf_op jit(solution)/shard_map/all_gather | solution.py:184
  579.8 9.5 %fusion.16 = bf16[1,128,1024]{2,1,0:T(8,128)(2,1)} fusion(bf16[128,8192]{1,0:T(8,128)(2,1)} %all-gather.8.cloned.1.call-done, bf16[8192,1024]{1,0:T(8,128)(2,1)} %all-gather.10.cloned.1.call-done), kind=kOutput, calls=%fused_computation.31 | convolution fusion | flops 2147614720 | bytes 19136512 | tf_op jit(solution)/shard_map/dot_general | solution.py:84
  (66 shorter events, 1.4 us)
Async XLA Ops:
  7.2 0.8 copy-start
  8.6 12.0 %all-to-all-start.2 = ((bf16[4,2,1024]{2,1,0:T(2,128)(2,1)}), bf16[4,2,1024]{2,1,0:T(2,128)(2,1)S(1)}, u32[]{:S(2)}, u32[]{:S(2)}) async-start(bf16[4,2,1024]{2,1,0:T(2,128)(2,1)} %reshape.457), calls=%async_computation.2 | async-start | bytes 32768 | tf_op jit(solution)/shard_map/all_to_all | solution.py:111
  19.3 7.5 %copy-start.10 = (f32[128]{0:T(128)}, f32[128]{0:T(128)S(1)}, u32[]{:S(2)}) copy-start(f32[128]{0:T(128)S(1)} %get-tuple-element.282) | copy-start | bytes 1540
  20.6 19.8 %all-to-all-start.1 = ((bf16[1,4,1,32,256]{4,3,2,0,1:T(8,128)(2,1)}), bf16[1,4,1,32,256]{4,3,2,0,1:T(8,128)(2,1)S(1)}, u32[]{:S(2)}, u32[]{:S(2)}) async-start(bf16[1,4,1,32,256]{4,3,2,0,1:T(8,128)(2,1)} %bitcast.147), calls=%async_computation.1 | async-start | bytes 131072 | tf_op jit(solution)/shard_map/all_to_all | solution.py:110
  28.9 15.8 %copy-start.5 = (f32[64]{0:T(128)S(1)}, f32[64]{0:T(128)}, u32[]{:S(2)}) copy-start(f32[64]{0:T(128)} %custom-call.1) | copy-start | bytes 772
  28.9 15.9 %copy-start.14 = (pred[128]{0:T(512)(128)(4,1)S(1)}, pred[128]{0:T(512)(128)(4,1)}, u32[]{:S(2)}) copy-start(pred[128]{0:T(512)(128)(4,1)} %get-tuple-element.283) | copy-start | bytes 388
  40.4 4.4 copy-start.4
  40.4 29.6 %copy-start.3 = (f32[128,4096]{1,0:T(8,128)S(1)}, f32[128,4096]{1,0:T(8,128)}, u32[]{:S(2)}) copy-start(f32[128,4096]{1,0:T(8,128)} %copy.80) | copy-start | bytes 6291460
  40.4 26.5 %all-to-all-start = ((bf16[1,4,1,32,4096]{4,3,2,0,1:T(8,128)(2,1)}), bf16[1,4,1,32,4096]{4,3,2,0,1:T(8,128)(2,1)S(1)}, u32[]{:S(2)}, u32[]{:S(2)}) async-start(bf16[1,4,1,32,4096]{4,3,2,0,1:T(8,128)(2,1)} %bitcast.137), calls=%async_computation | async-start | bytes 2097152 | tf_op jit(solution)/shard_map/all_to_all | solution.py:108
  44.1 198.5 %all-gather.12.cloned.1.call-start = ((), (), s32[]{:S(2)}) async-start(), calls=%async_computation.6 | async-start | bytes 10485760 | tf_op jit(solution)/shard_map/all_gather | solution.py:23
  44.8 22.1 %copy-start.6 = (f32[64]{0:T(128)}, f32[64]{0:T(128)S(1)}, u32[]{:S(2)}) copy-start(f32[64]{0:T(128)S(1)} %get-tuple-element.224) | copy-start | bytes 772
  44.8 22.1 %copy-start.9 = (f32[4,64]{1,0:T(4,128)}, f32[4,64]{1,0:T(4,128)S(1)}, u32[]{:S(2)}) copy-start(f32[4,64]{1,0:T(4,128)S(1)} %get-tuple-element.430) | copy-start | bytes 3076
  46.4 22.1 %collective-permute-start.1 = (bf16[3,256]{1,0:T(4,128)(2,1)S(1)}, bf16[3,256]{1,0:T(4,128)(2,1)S(1)}, u32[]{:S(2)}, u32[]{:S(2)}) collective-permute-start(bf16[3,256]{1,0:T(4,128)(2,1)S(1)} %get-tuple-element.287), channel_id=1, source_target_pairs={{0,4},{4,8},{8,12},{1,5},{5,9},{9,13},{2,6},{6,10},{10,14},{3,7},{... | collective-permute-start | bytes 4616 | tf_op jit(solution)/shard_map/ppermute | solution.py:18
  67.2 2.9 collective-permute-start
  68.5 0.6 copy-start.15
  73.1 1.6 copy-start.7
  73.1 1.6 copy-start.16
  77.2 317.1 %all-gather.14.cloned.1.call-start = ((), (), s32[]{:S(2)}) async-start(), calls=%async_computation.7 | async-start | bytes 10485760 | tf_op jit(solution)/shard_map/all_gather | solution.py:174
  77.3 6.4 %copy-start.11 = (f32[128]{0:T(128)S(1)}, f32[128]{0:T(128)}, u32[]{:S(2)}) copy-start(f32[128]{0:T(128)} %copy-done.10) | copy-start | bytes 1540
  77.3 6.4 %copy-start.13 = (f32[64]{0:T(128)S(1)}, f32[64]{0:T(128)}, u32[]{:S(2)}) copy-start(f32[64]{0:T(128)} %param.22) | copy-start | bytes 772
  78.0 54.5 %all-to-all-start.3 = ((bf16[1,4,1,32,4096]{4,3,2,0,1:T(8,128)(2,1)}), bf16[1,4,1,32,4096]{4,3,2,0,1:T(8,128)(2,1)}, u32[]{:S(2)}, u32[]{:S(2)}) async-start(bf16[1,4,1,32,4096]{4,3,2,0,1:T(8,128)(2,1)} %bitcast.35), calls=%async_computation.3 | async-start | bytes 2097152 | tf_op jit(solution)/shard_map/all_to_all | solution.py:109
  83.7 343.6 %all-gather.8.cloned.1.call-start = ((), (), s32[]{:S(2)}) async-start(), calls=%async_computation.4 | async-start | bytes 3145728 | tf_op jit(solution)/shard_map/all_gather | solution.py:182
  242.6 11.7 %copy-start.17 = (f32[64]{0:T(128)S(1)}, f32[64]{0:T(128)}, u32[]{:S(2)}) copy-start(f32[64]{0:T(128)} %param.23) | copy-start | bytes 772
  260.6 8.0 %copy-start.2 = (f32[1,4,1,32,4096]{4,3,1,2,0:T(8,128)S(1)}, f32[1,4,1,32,4096]{4,3,1,2,0:T(8,128)}, u32[]{:S(2)}) copy-start(f32[1,4,1,32,4096]{4,3,1,2,0:T(8,128)} %bitcast_convert_fusion) | copy-start | bytes 6291460
  260.7 8.0 %copy-start.8 = (f32[4096]{0:T(1024)S(1)}, f32[4096]{0:T(1024)}, u32[]{:S(2)}) copy-start(f32[4096]{0:T(1024)} %param.26) | copy-start | bytes 49156
  271.9 0.7 copy-start.18
  271.9 3.2 copy-start.12
  271.9 307.9 %all-gather.10.cloned.1.call-start = ((), (), s32[]{:S(2)}) async-start(), calls=%async_computation.5 | async-start | bytes 18874368 | tf_op jit(solution)/shard_map/all_gather | solution.py:184
  579.8 9.5 %copy-start.1 = (bf16[1,4,1,32,64]{4,3,2,1,0:T(8,128)(2,1)S(1)}, bf16[1,4,1,32,64]{4,3,2,1,0:T(8,128)(2,1)}, u32[]{:S(2)}) copy-start(bf16[1,4,1,32,64]{4,3,2,1,0:T(8,128)(2,1)} %param.20) | copy-start | bytes 49156
Sparse Core Ops, SparseCore 0:
  77.4 165.1 all-gather.11
  244.1 150.1 all-gather.13
  395.9 31.3 all-gather.7
  428.7 151.0 all-gather.9
